TPU v7x, 128 devices: a whole 4x4x4 slice. The times are simulated.
128 devices in a mesh: row: 4 (over z_hi, core), col: 8 (over z_lo, x), depth: 4 (over y).
Axes of the slice: x: 4, y: 4, z: 4 (z_hi: 2, z_lo: 2; z = z_hi * 2 + z_lo), core: 2. Of those that a mesh axis runs over, the one named last changes fastest.
Arguments:
- pair_input: bfloat16 [768, 768, 128], P('row', ('col', 'depth')), may hold values from -40 to 40
- in_gain: float32 [128], replicated, may hold values from 0.1 to 1.9
- in_shift: float32 [128], replicated, may hold values from -3 to 3
- w_proj: bfloat16 [128, 512], replicated, may hold values from -0.5 to 0.5
- w_gate: bfloat16 [128, 128], replicated, may hold values from -0.5 to 0.5
- out_gain: float32 [128], replicated, may hold values from 0.1 to 1.9
- out_shift: float32 [128], replicated, may hold values from -3 to 3
- w_out: bfloat16 [128, 128], replicated, may hold values from -0.5 to 0.5
Outputs:
- update: bfloat16 [768, 768, 128], P('row', ('col', 'depth'))
All inputs are finite; a program needn't handle non-finite values.
Results may differ from a plain program's by a relative error of at most 0.013.
Values may be sent and summed in bfloat16 or wider, within the bound.
A program may use at most 64 MiB of HBM per device.

v0:
```python
import jax
import jax.numpy as jnp
from jax import lax
from jax.sharding import PartitionSpec as P


def cut_along(array, dim, length):
    before, after = (array.shape[:dim], array.shape[dim + 1 :])
    return jnp.moveaxis(array.reshape(*before, length, -1, *after), dim, 0)


def in_order(parts, dim):
    parts = jnp.moveaxis(parts, 0, dim)
    dims = parts.shape
    return parts.reshape(*dims[:dim], dims[dim] * dims[dim + 1], *dims[dim + 2 :])


def joined_exchange(array, axis, axes, splits, concats):
    sizes = [lax.axis_size(a) for a in axes]
    parts = cut_along(array, splits[0], sizes[0])
    parts = jnp.moveaxis(cut_along(parts, splits[1] + 1, sizes[1]), 0, 1)
    inside = parts.shape[2:]
    parts = parts.reshape(-1, *inside)
    parts = lax.all_to_all(parts, axis, split_axis=0, concat_axis=0, tiled=True)
    parts = in_order(parts.reshape(*sizes, *inside), concats[0] + 1)
    return in_order(parts, concats[1])


def layer_norm(values, scaling, offsets):
    average = jnp.mean(values, axis=-1, keepdims=True)
    centred = values - average
    variance = jnp.mean(centred * centred, axis=-1, keepdims=True)
    return centred * lax.rsqrt(variance + 1e-05) * scaling + offsets


def gated_sides(normed, w_proj):
    channels = w_proj.shape[1] // 4
    projected = jnp.einsum("xyc,cd->xyd", normed, w_proj, preferred_element_type=jnp.float32)
    left_side = (
        jax.nn.sigmoid(projected[..., :channels]) * projected[..., channels : 2 * channels]
    ).astype(jnp.bfloat16)
    right_side = (
        jax.nn.sigmoid(projected[..., 2 * channels : 3 * channels]) * projected[..., 3 * channels :]
    ).astype(jnp.bfloat16)
    return (left_side, right_side)


def reorder_channels(values, row_count, other_count):
    shape_rest = values.shape[1:]
    grouped = values.reshape((row_count, other_count, -1) + shape_rest)
    return jnp.swapaxes(grouped, 0, 1).reshape(values.shape)


def per_device(pair_input, in_gain, in_shift, w_proj, w_gate, out_gain, out_shift, w_out):
    row_count = lax.axis_size("row")
    col_count = lax.axis_size("col")
    depth_count = lax.axis_size("depth")
    normed = layer_norm(pair_input.astype(jnp.float32), in_gain, in_shift).astype(jnp.bfloat16)
    left_side, right_side = gated_sides(normed, w_proj)
    left_all, right_all = (
        joined_exchange(
            left_side, ("row", "col", "depth"), ("row", ("col", "depth")), (2, 2), (0, 1)
        ),
        joined_exchange(
            right_side, ("row", "col", "depth"), ("row", ("col", "depth")), (2, 2), (0, 1)
        ),
    )
    planes = jnp.einsum("kic,kjc->ijc", left_all, right_all, preferred_element_type=jnp.float32)
    product = joined_exchange(
        planes.astype(jnp.bfloat16),
        ("row", "col", "depth"),
        ("row", ("col", "depth")),
        (0, 1),
        (2, 2),
    ).astype(planes.dtype)
    other_count = col_count * depth_count
    used_gain = reorder_channels(out_gain, row_count, other_count)
    used_shift = reorder_channels(out_shift, row_count, other_count)
    used_out = reorder_channels(w_out, row_count, other_count)
    product_norm = layer_norm(product, used_gain, used_shift).astype(jnp.bfloat16)
    gating = jax.nn.sigmoid(
        jnp.einsum("xyc,cd->xyd", normed, w_gate, preferred_element_type=jnp.float32)
    )
    projected_out = jnp.einsum(
        "xyc,cd->xyd", product_norm, used_out, preferred_element_type=jnp.float32
    )
    return (gating * projected_out).astype(jnp.bfloat16)


def solution(mesh):
    placed = (P("row", ("col", "depth"), None), P(), P(), P(), P(), P(), P(), P())
    return jax.shard_map(
        per_device,
        mesh=mesh,
        in_specs=placed,
        out_specs=P("row", ("col", "depth"), None),
        check_vma=False,
    )
```

profile of v0, /device:TPU:1, one launch (start us, length us, event | category | flops | bytes accessed | tf_op | source)
XLA Modules:
  0.0 127.2 jit_solution(3613307496950191818)
XLA Ops:
  0.0 2.1 %convert_reduce_fusion = f32[192,24]{1,0:T(8,128)S(1)} fusion(bf16[192,24,128]{2,1,0:T(8,128)(2,1)} %param.8), kind=kLoop, calls=%fused_computation.9 | loop fusion | flops 1175040 | bytes 1198080 | tf_op jit(solution)/shard_map/reduce_sum | solution.py:30
  2.2 0.1 copy.59
  2.3 1.4 %fusion.8 = f32[192,24]{1,0:T(8,128)S(1)} fusion(bf16[192,24,128]{2,1,0:T(8,128)(2,1)S(1)} %copy-done.1, f32[192,24]{1,0:T(8,128)S(1)} %copy.59), kind=kLoop, calls=%fused_computation.12 | loop fusion | flops 2354688 | bytes 1216512 | tf_op jit(solution)/shard_map/reduce_sum | solution.py:32
  3.8 0.1 copy.61
  3.9 1.6 %fusion.21 = f32[192,24,512]{2,1,0:T(8,128)S(1)} fusion(bf16[192,24,128]{2,1,0:T(8,128)(2,1)S(1)} %copy-done.1, f32[128]{0:T(128)S(1)} %copy-done.3, f32[128]{0:T(128)S(1)} %copy-done.4, f32[192,24]{1,0:T(8,128)S(1)} %copy.61, f32[192,24]{1,0:T(8,128)S(1)} %copy.59, bf16[128,512]{1,0:T(8,128)(2,1)S(1)} %copy-done), kind=kOutput, calls=%fused_computation.31 | convolution fusion | flops 607518720 | bytes 10785792 | tf_op jit(solution)/shard_map/xyc,cd->xyd/dot_general | solution.py:38
  5.6 2.6 %fusion.12 = (bf16[192,24,128]{2,1,0:T(8,128)(2,1)}, bf16[192,24,128]{2,1,0:T(8,128)(2,1)}) fusion(f32[192,24,512]{2,1,0:T(8,128)S(1)} %fusion.21), kind=kLoop, calls=%fused_computation.17 | loop fusion | flops 5898240 | bytes 11796480 | tf_op jit(solution)/shard_map/convert_element_type | solution.py:41
  8.2 2.1 %copy.62 = bf16[192,24,128]{0,2,1:T(8,128)(2,1)S(1)} copy(bf16[192,24,128]{2,1,0:T(8,128)(2,1)} %get-tuple-element.6) | data formatting | bytes 2359296 | tf_op jit(solution)/shard_map/convert_element_type | solution.py:44
  10.3 2.0 %copy.64 = bf16[128,192,24,1]{1,2,3,0:T(8,128)(2,1)} copy(bf16[128,192,24,1]{1,0,2,3:T(8,128)(2,1)S(1)} %bitcast.96) | data formatting | bytes 2359296 | tf_op jit(solution)/shard_map/reshape | solution.py:23
  12.4 11.5 %all-to-all-start = ((bf16[128,192,24,1]{1,2,3,0:T(8,128)(2,1)}), bf16[128,192,24,1]{1,2,3,0:T(8,128)(2,1)S(1)}, u32[]{:S(2)}, u32[]{:S(2)}) async-start(bf16[128,192,24,1]{1,2,3,0:T(8,128)(2,1)} %copy.64), calls=%async_computation | async-start | bytes 3145728 | tf_op jit(solution)/shard_map/all_to_all | solution.py:24
  23.9 2.9 %copy.66 = bf16[192,24,128]{0,2,1:T(8,128)(2,1)} copy(bf16[192,24,128]{2,1,0:T(8,128)(2,1)} %get-tuple-element.5) | data formatting | bytes 2359296 | tf_op jit(solution)/shard_map/convert_element_type | solution.py:41
  26.8 3.5 %copy.68 = bf16[128,192,24,1]{1,2,3,0:T(8,128)(2,1)} copy(bf16[128,192,24,1]{1,0,2,3:T(8,128)(2,1)} %bitcast.97) | data formatting | bytes 2359296 | tf_op jit(solution)/shard_map/reshape | solution.py:23
  30.2 17.5 %all-to-all-done = bf16[128,192,24,1]{1,2,3,0:T(8,128)(2,1)S(1)} async-done(((bf16[128,192,24,1]{1,2,3,0:T(8,128)(2,1)}), bf16[128,192,24,1]{1,2,3,0:T(8,128)(2,1)S(1)}, u32[]{:S(2)}, u32[]{:S(2)}) %all-to-all-start) | async-done | bytes 1179680 | tf_op jit(solution)/shard_map/all_to_all | solution.py:24
  47.7 6.1 %all-to-all-start.1 = ((bf16[128,192,24,1]{1,2,3,0:T(8,128)(2,1)}), bf16[128,192,24,1]{1,2,3,0:T(8,128)(2,1)}, u32[]{:S(2)}, u32[]{:S(2)}) async-start(bf16[128,192,24,1]{1,2,3,0:T(8,128)(2,1)} %copy.68), calls=%async_computation.1 | async-start | bytes 3145728 | tf_op jit(solution)/shard_map/all_to_all | solution.py:24
  53.9 2.4 %copy.65 = bf16[32,4,192,24,1]{2,1,3,0,4:T(4,128)(2,1)} copy(bf16[32,4,192,24,1]{2,3,0,1,4:T(8,128)(2,1)S(1)} %bitcast.94) | data formatting | bytes 2359296 | tf_op jit(solution)/shard_map/transpose | solution.py:13
  56.2 4.0 %reshape.101 = bf16[32,768,24,1]{1,2,0,3:T(8,128)(2,1)} reshape(bf16[32,4,192,24,1]{2,1,3,0,4:T(4,128)(2,1)} %copy.65) | data formatting | bytes 2359296 | tf_op jit(solution)/shard_map/reshape | solution.py:15
  60.2 17.3 %all-to-all-done.1 = bf16[128,192,24,1]{1,2,3,0:T(8,128)(2,1)} async-done(((bf16[128,192,24,1]{1,2,3,0:T(8,128)(2,1)}), bf16[128,192,24,1]{1,2,3,0:T(8,128)(2,1)}, u32[]{:S(2)}, u32[]{:S(2)}) %all-to-all-start.1) | async-done | bytes 1179680 | tf_op jit(solution)/shard_map/all_to_all | solution.py:24
  77.5 2.6 %copy.69 = bf16[32,4,192,24,1]{2,1,3,0,4:T(4,128)(2,1)S(1)} copy(bf16[32,4,192,24,1]{2,3,0,1,4:T(8,128)(2,1)} %bitcast.17) | data formatting | bytes 2359296 | tf_op jit(solution)/shard_map/transpose | solution.py:13
  80.2 2.2 %reshape.107 = bf16[32,768,24,1]{1,2,0,3:T(8,128)(2,1)} reshape(bf16[32,4,192,24,1]{2,1,3,0,4:T(4,128)(2,1)S(1)} %copy.69) | data formatting | bytes 2359296 | tf_op jit(solution)/shard_map/reshape | solution.py:15
  82.4 3.8 %fusion.20 = bf16[768,768,1]{0,1,2:T(8,128)(2,1)} fusion(bf16[768,768]{0,1:T(8,128)(2,1)} %bitcast.99, bf16[768,768]{0,1:T(8,128)(2,1)} %bitcast.100), kind=kOutput, calls=%fused_computation.30 | convolution fusion | flops 906559488 | bytes 3538944 | tf_op jit(solution)/shard_map/kic,kjc->ijc/dot_general | solution.py:68
  86.2 3.5 %reshape_reshape.3 = bf16[4,192,32,24,1]{1,0,3,2,4:T(4,128)(2,1)S(1)} reshape(bf16[768,768,1]{0,1,2:T(8,128)(2,1)} %fusion.20) | data formatting | bytes 2359296 | tf_op jit(solution)/shard_map/reshape;reshape | solution.py:9
  89.7 1.4 %copy.70 = bf16[4,192,32,24,1]{1,3,2,0,4:T(8,128)(2,1)} copy(bf16[4,192,32,24,1]{1,0,3,2,4:T(4,128)(2,1)S(1)} %reshape_reshape.3) | data formatting | bytes 2359296 | tf_op jit(solution)/shard_map/reshape;reshape | solution.py:9
  91.0 5.3 %all-to-all-start.2 = ((bf16[128,192,24,1]{1,2,3,0:T(8,128)(2,1)}), bf16[128,192,24,1]{1,2,3,0:T(8,128)(2,1)S(1)}, u32[]{:S(2)}, u32[]{:S(2)}) async-start(bf16[128,192,24,1]{1,2,3,0:T(8,128)(2,1)} %bitcast.95), calls=%async_computation.2 | async-start | bytes 3145728 | tf_op jit(solution)/shard_map/all_to_all | solution.py:24
  96.3 0.1 reshape.110
  96.4 0.1 reshape.111
  96.5 3.1 %fusion.23 = f32[192,24,128]{2,1,0:T(8,128)} fusion(bf16[192,24,128]{2,1,0:T(8,128)(2,1)S(1)} %copy-done.1, f32[128]{0:T(128)S(1)} %copy-done.3, f32[128]{0:T(128)S(1)} %copy-done.4, f32[192,24]{1,0:T(8,128)S(1)} %copy.61, f32[192,24]{1,0:T(8,128)S(1)} %copy.59, bf16[128,128]{1,0:T(8,128)(2,1)S(1)} %copy-done.7), kind=kOutput, calls=%fused_computation.32 | convolution fusion | flops 154533888 | bytes 3609600 | tf_op jit(solution)/shard_map/xyc,cd->xyd/dot_general | solution.py:82
  99.6 20.7 %all-to-all-done.2 = bf16[128,192,24,1]{1,2,3,0:T(8,128)(2,1)S(1)} async-done(((bf16[128,192,24,1]{1,2,3,0:T(8,128)(2,1)}), bf16[128,192,24,1]{1,2,3,0:T(8,128)(2,1)S(1)}, u32[]{:S(2)}, u32[]{:S(2)}) %all-to-all-start.2) | async-done | bytes 1179680 | tf_op jit(solution)/shard_map/all_to_all | solution.py:24
  120.3 0.3 bitcast_reduce_fusion
  120.6 0.5 fusion.2
  121.1 0.6 fusion.5
  121.7 0.2 copy.73
  121.9 1.7 %copy.75 = bf16[192,24,128]{2,1,0:T(8,128)(2,1)S(1)} copy(bf16[192,24,128]{0,1,2:T(8,128)(2,1)S(1)} %bitcast.98) | data formatting | bytes 2359296 | tf_op jit(solution)/shard_map/convert_element_type | solution.py:80
  123.7 3.5 %multiply_convert_fusion = bf16[192,24,128]{2,1,0:T(8,128)(2,1)} fusion(f32[192,24,128]{2,1,0:T(8,128)} %fusion.23, bf16[192,24,128]{2,1,0:T(8,128)(2,1)S(1)} %copy.75, bf16[128,128,1]{1,0,2:T(8,128)(2,1)S(1)} %bitcast.102), kind=kOutput, calls=%fused_computation.28 | convolution fusion | flops 153944064 | bytes 4751360 | tf_op jit(solution)/shard_map/xyc,cd->xyd/dot_general | solution.py:84
  (23 shorter events, 0.2 us)
Async XLA Ops:
  0.0 3.9 %copy-start = (bf16[128,512]{1,0:T(8,128)(2,1)S(1)}, bf16[128,512]{1,0:T(8,128)(2,1)}, u32[]{:S(2)}) copy-start(bf16[128,512]{1,0:T(8,128)(2,1)} %param.11) | copy-start | bytes 393220
  0.0 2.3 %copy-start.1 = (bf16[192,24,128]{2,1,0:T(8,128)(2,1)S(1)}, bf16[192,24,128]{2,1,0:T(8,128)(2,1)}, u32[]{:S(2)}) copy-start(bf16[192,24,128]{2,1,0:T(8,128)(2,1)} %param.8) | copy-start | bytes 3538948
  0.0 3.9 %copy-start.3 = (f32[128]{0:T(128)S(1)}, f32[128]{0:T(128)}, u32[]{:S(2)}) copy-start(f32[128]{0:T(128)} %param.10) | copy-start | bytes 1540
  0.0 3.9 %copy-start.4 = (f32[128]{0:T(128)S(1)}, f32[128]{0:T(128)}, u32[]{:S(2)}) copy-start(f32[128]{0:T(128)} %param.9) | copy-start | bytes 1540
  12.4 35.3 %all-to-all-start = ((bf16[128,192,24,1]{1,2,3,0:T(8,128)(2,1)}), bf16[128,192,24,1]{1,2,3,0:T(8,128)(2,1)S(1)}, u32[]{:S(2)}, u32[]{:S(2)}) async-start(bf16[128,192,24,1]{1,2,3,0:T(8,128)(2,1)} %copy.64), calls=%async_computation | async-start | bytes 3145728 | tf_op jit(solution)/shard_map/all_to_all | solution.py:24
  47.7 29.8 %all-to-all-start.1 = ((bf16[128,192,24,1]{1,2,3,0:T(8,128)(2,1)}), bf16[128,192,24,1]{1,2,3,0:T(8,128)(2,1)}, u32[]{:S(2)}, u32[]{:S(2)}) async-start(bf16[128,192,24,1]{1,2,3,0:T(8,128)(2,1)} %copy.68), calls=%async_computation.1 | async-start | bytes 3145728 | tf_op jit(solution)/shard_map/all_to_all | solution.py:24
  91.0 5.3 %copy-start.5 = (f32[128]{0:T(128)S(1)}, f32[128]{0:T(128)}, u32[]{:S(2)}) copy-start(f32[128]{0:T(128)} %param.13) | copy-start | bytes 1540
  91.0 5.4 %copy-start.6 = (f32[128]{0:T(128)S(1)}, f32[128]{0:T(128)}, u32[]{:S(2)}) copy-start(f32[128]{0:T(128)} %param.14) | copy-start | bytes 1540
  91.0 5.5 %copy-start.2 = (bf16[128,128]{1,0:T(8,128)(2,1)S(1)}, bf16[128,128]{1,0:T(8,128)(2,1)}, u32[]{:S(2)}) copy-start(bf16[128,128]{1,0:T(8,128)(2,1)} %param.15) | copy-start | bytes 98308
  91.0 5.5 %copy-start.7 = (bf16[128,128]{1,0:T(8,128)(2,1)S(1)}, bf16[128,128]{1,0:T(8,128)(2,1)}, u32[]{:S(2)}) copy-start(bf16[128,128]{1,0:T(8,128)(2,1)} %param.12) | copy-start | bytes 98308
  91.0 29.3 %all-to-all-start.2 = ((bf16[128,192,24,1]{1,2,3,0:T(8,128)(2,1)}), bf16[128,192,24,1]{1,2,3,0:T(8,128)(2,1)S(1)}, u32[]{:S(2)}, u32[]{:S(2)}) async-start(bf16[128,192,24,1]{1,2,3,0:T(8,128)(2,1)} %bitcast.95), calls=%async_computation.2 | async-start | bytes 3145728 | tf_op jit(solution)/shard_map/all_to_all | solution.py:24
where the time goes:
time: 128 us; the launch traced here: 127 us
  waiting for transfers between devices  55.5 us (43%)
  local copies, waits for them, and re-layouts  29.1 us (23%)
  starting transfers between devices  22.9 us (18%)
  matrix products  12 us (9%)
  other arithmetic  7.58 us (6%)
    all_to_all x3, waiting for transfers between devices, joined_exchange(): parts = lax.all_to_all(parts, axis, split_axis=0, concat_axis=0, tiled=True)  55.5 us
    all_to_all x3, starting transfers between devices, joined_exchange(): parts = lax.all_to_all(parts, axis, split_axis=0, concat_axis=0, tiled=True)  22.9 us
    reshape x2, local copies, waits for them, and re-layouts, in_order(): parts.reshape(*dims[:dim], dims[dim] * dims[dim + 1], *dims[dim + 2:])  6.26 us
    reshape x2, local copies, waits for them, and re-layouts, joined_exchange(): parts = parts.reshape(-1, *inside)  5.49 us
    transpose x2, local copies, waits for them, and re-layouts, in_order(): parts = jnp.moveaxis(parts, 0, dim)  4.99 us
    another operation x2, local copies, waits for them, and re-layouts, cut_along(): return jnp.moveaxis(array.reshape(*before, length, -1, *after), dim, 0)  4.83 us
    dot_general x1, matrix products, per_device(): jnp.einsum('kic,kjc->ijc', left_all, right_all, preferred_element_type=jn...  3.78 us
    dot_general x1, matrix products, per_device(): jnp.einsum('xyc,cd->xyd', product_norm, used_out, preferred_element_type=...  3.48 us
  transfers between devices with their start and end apart: 3, of which 3 were waited for; matrix products, arithmetic and copies ran while one was open for 13% of the time, Pallas kernels for 0%

commit v1 on v0

v1 whole, which is shorter than its diff:
```python
import functools

import jax
import jax.numpy as jnp
from jax import lax
from jax.experimental import pallas as pl
from jax.experimental.pallas import tpu as pltpu
from jax.sharding import PartitionSpec as P

BF = jnp.bfloat16
F32 = jnp.float32
EPS = 1e-05


def div(a, b):
    return lax.div(a, jnp.int32(b))


def rem(a, b):
    return lax.rem(a, jnp.int32(b))


def dot_nt(a, b):
    return lax.dot_general(a, b, (((1,), (1,)), ((), ())), preferred_element_type=F32)


def kernel(
    x_ref, ig_ref, is_ref, wp_ref, wg_ref, og_ref, os_ref, wo_ref, out_ref,
    xin, xs, wsel, lsend, rsend, stage, recv_l, recv_r, psend, recv_p, peer_p,
    gate, pn, ostage, obf,
    own_sem, x_send, x_recv, l_send, l_recv, r_send, r_recv, p_send, p_recv, e_send, e_recv, o_sem,
):
    row = lax.axis_index("row")
    col = lax.axis_index("col")
    y = lax.axis_index("depth")
    zh, core = div(row, 2), rem(row, 2)
    zl, x = div(col, 4), rem(col, 4)
    q = col * 4 + y
    me = zh * 32 + q
    other = {"row": zh * 2 + 1 - core, "col": col, "depth": y}
    low = pl.multiple_of(zh * 384, 128)

    def chip(o):
        zh2 = rem(zh + div(o, 32), 2)
        zl2 = rem(zl + div(o, 16), 2)
        x2 = rem(x + div(o, 4), 4)
        y2 = rem(y + o, 4)
        col2 = zl2 * 4 + x2
        q2 = col2 * 4 + y2
        return zh2, q2, zh2 * 32 + q2, {"row": zh2 * 2 + core, "col": col2, "depth": y2}

    def own_copy(t, u):
        start = core * 128 + u * 64 if u < 2 else 256 + core * 64
        return pltpu.make_async_copy(
            x_ref.at[:, u, :, pl.ds(t * 8, 8), :], xin.at[t, pl.ds(div(start, 8), 8)], own_sem.at[t]
        )

    for t in range(3):
        for u in range(3):
            own_copy(t, u).start()

    barrier = pltpu.get_barrier_semaphore()
    pl.semaphore_signal(barrier, inc=1, device_id=other)

    def greet(o, carry):
        pl.semaphore_signal(barrier, inc=1, device_id=chip(o)[3])
        return carry

    lax.fori_loop(1, 64, greet, 0)

    for part in range(4):
        block = wp_ref[:, part * 128 : (part + 1) * 128].astype(F32).T
        stage[0, 0:128, :] = block
        wsel[part * 64 : (part + 1) * 64, :] = stage[0, pl.ds(pl.multiple_of(core * 64, 64), 64), :].astype(BF)

    pl.semaphore_wait(barrier, 64)

    def peer_copy(t, u):
        start = core * 128 + u * 64 if u < 2 else 256 + core * 64
        return pltpu.make_async_remote_copy(
            src_ref=x_ref.at[:, u, :, pl.ds(t * 8, 8), :],
            dst_ref=xin.at[t, pl.ds(div(start, 8), 8)],
            send_sem=x_send,
            recv_sem=x_recv.at[t],
            device_id=other,
        )

    for t in range(3):
        for u in range(3):
            peer_copy(t, u).start()

    in_gain = ig_ref[...]
    in_shift = is_ref[...]

    def norm_rows(t):
        def chunk(i, carry):
            v = xin[t, pl.ds(i * 4, 4)].astype(F32)
            v = v - jnp.mean(v, axis=-1, keepdims=True)
            v = v * lax.rsqrt(jnp.mean(v * v, axis=-1, keepdims=True) + EPS)
            v = v * in_gain.reshape(1, 1, 1, 128) + in_shift.reshape(1, 1, 1, 128)
            xs[pl.ds(pl.multiple_of(t * 3072 + i * 256, 256), 256), :] = v.reshape(256, 128)
            return carry

        lax.fori_loop(0, 12, chunk, 0)

    def project(t, base, dst):
        w = wsel[base : base + 128, :]
        for i in range(8):
            rows = xs[pl.ds(t * 3072 + i, 384, stride=8), :].astype(BF)
            p = dot_nt(w, rows)
            side = jax.nn.sigmoid(p[0:64]) * p[64:128]
            for c in range(3):
                stage[c, pl.ds(i, 64, stride=8), :] = side[:, c * 128 : (c + 1) * 128]
        for c in range(3):
            dst[pl.ds(t * 64, 64), :, c * 128 : (c + 1) * 128] = stage[c].reshape(64, 8, 128).astype(BF)

    def left(t, carry):
        pltpu.make_async_copy(xin.at[t, pl.ds(0, 24)], xin.at[t, pl.ds(0, 24)], own_sem.at[t]).wait()
        pltpu.make_async_copy(xin.at[t, pl.ds(0, 24)], xin.at[t, pl.ds(0, 24)], x_recv.at[t]).wait()
        norm_rows(t)
        project(t, 0, lsend)
        late = div(t, 2)
        group = div(q, 16) * 48 + rem(div(q, 8), 2) * (16 - 8 * late) + t * 8 * (1 - late) + 32 * late + rem(q, 8)

        def send(o, carry):
            _, _, n, device = chip(o)
            pltpu.make_async_remote_copy(
                src_ref=lsend.at[t * 64 + n],
                dst_ref=recv_l.at[group, :, pl.ds(low, 384)],
                send_sem=l_send,
                recv_sem=l_recv,
                device_id=device,
            ).start()
            return carry

        lax.fori_loop(1, 64, send, 0)
        recv_l[group, :, pl.ds(low, 384)] = lsend[t * 64 + me]
        return carry

    lax.fori_loop(0, 3, left, 0)

    def right(t, carry):
        project(t, 128, rsend)

        def send(o, carry):
            _, _, n, device = chip(o)
            pltpu.make_async_remote_copy(
                src_ref=rsend.at[t * 64 + n],
                dst_ref=recv_r.at[t * 32 + q, :, pl.ds(low, 384)],
                send_sem=r_send,
                recv_sem=r_recv.at[t],
                device_id=device,
            ).start()
            return carry

        lax.fori_loop(1, 64, send, 0)
        recv_r[t * 32 + q, :, pl.ds(low, 384)] = rsend[t * 64 + me]
        return carry

    lax.fori_loop(0, 3, right, 0)

    def gates(t, carry):
        w = wg_ref[...]
        for i in range(8):
            a = xs[pl.ds(t * 3072 + core * 1024 + i, 128, stride=8), :].astype(BF)
            b = xs[pl.ds(t * 3072 + 2048 + core * 512 + i, 64, stride=8), :].astype(BF)
            rows = jnp.concatenate([a, b], axis=0)
            gate[t * 8 + i] = jax.nn.sigmoid(jnp.dot(rows, w, preferred_element_type=F32))
        return carry

    lax.fori_loop(0, 3, gates, 0)

    pltpu.make_async_copy(lsend.at[pl.ds(0, 189)], lsend.at[pl.ds(0, 189)], l_recv).wait()

    def product(t, carry):
        pltpu.make_async_copy(rsend.at[pl.ds(0, 63)], rsend.at[pl.ds(0, 63)], r_recv.at[t]).wait()
        rows = recv_r[pl.ds(t * 32, 32)].reshape(256, 768)
        for part in range(3):
            cols = recv_l[pl.ds(part * 32, 32)].reshape(256, 768)
            psend[pl.ds(t * 32, 32), :, part * 256 : (part + 1) * 256] = (
                dot_nt(rows, cols).astype(BF).reshape(32, 8, 256)
            )

        def send(o, carry):
            zh2, q2, _, device = chip(o)
            pltpu.make_async_remote_copy(
                src_ref=psend.at[t * 32 + q2, :, pl.ds(pl.multiple_of(zh2 * 384, 128), 384)],
                dst_ref=recv_p.at[t * 64 + me],
                send_sem=p_send,
                recv_sem=p_recv.at[t],
                device_id=device,
            ).start()
            return carry

        lax.fori_loop(1, 64, send, 0)
        recv_p[t * 64 + me] = psend[t * 32 + q, :, pl.ds(low, 384)]
        return carry

    lax.fori_loop(0, 3, product, 0)

    def to_peer(t, half):
        lane = pl.multiple_of((1 - core) * 128, 128) if half == 0 else 256
        return pltpu.make_async_remote_copy(
            src_ref=recv_p.at[pl.ds(t * 64, 64), :, pl.ds(lane, 128)],
            dst_ref=peer_p.at[pl.ds(t * 64, 64), :, pl.ds(half * 128, 128)],
            send_sem=e_send,
            recv_sem=e_recv.at[t],
            device_id=other,
        )

    own_lane = pl.multiple_of(core * 128, 128)
    first = core == 0
    out_gain = jnp.where(first, og_ref[...], pltpu.roll(og_ref[...], 64, 1))
    out_shift = jnp.where(first, os_ref[...], pltpu.roll(os_ref[...], 64, 1))

    def out_copy(t, u):
        return pltpu.make_async_copy(
            obf.at[pl.ds(u * 8, 8), :, pl.ds(t * 8, 8), :], out_ref.at[:, u, :, pl.ds(t * 8, 8), :], o_sem
        )

    def finish(t, carry):
        pltpu.make_async_copy(rsend.at[pl.ds(0, 63)], rsend.at[pl.ds(0, 63)], p_recv.at[t]).wait()
        to_peer(t, 0).start()
        to_peer(t, 1).start()
        pltpu.make_async_copy(
            peer_p.at[pl.ds(0, 64)], peer_p.at[pl.ds(0, 64)], e_recv.at[t]
        ).wait()

        def parts(lo, size):
            here = pl.ds(t * 64 + lo, size)
            return (
                jnp.concatenate(
                    [recv_p[here, :, pl.ds(own_lane, 128)], recv_p[here, :, 256:384]], axis=-1
                ).astype(F32),
                peer_p[here].astype(F32),
            )

        total = jnp.zeros((8, 256), F32)
        for lo in range(0, 64, 16):
            a, b = parts(lo, 16)
            total = total + (jnp.sum(a, axis=0) + jnp.sum(b, axis=0))
        average = total * (1.0 / 128.0)
        total = jnp.zeros((8, 256), F32)
        for lo in range(0, 64, 16):
            a, b = parts(lo, 16)
            a, b = a - average[None], b - average[None]
            total = total + (jnp.sum(a * a, axis=0) + jnp.sum(b * b, axis=0))
        scale = lax.rsqrt(total * (1.0 / 128.0) + EPS)
        for lo in range(0, 64, 16):
            a, b = parts(lo, 16)
            a = ((a - average[None]) * scale[None]).reshape(128, 256)
            b = ((b - average[None]) * scale[None]).reshape(128, 256)
            for c in range(2):
                pn[c, lo * 8 : lo * 8 + 128, :] = a[:, c * 128 : (c + 1) * 128]
                pn[c, 512 + lo * 8 : 512 + lo * 8 + 128, :] = b[:, c * 128 : (c + 1) * 128]
        w_own = wo_ref[pl.ds(pl.multiple_of(core * 64, 64), 64), :]
        w_other = wo_ref[pl.ds(pl.multiple_of((1 - core) * 64, 64), 64), :]
        w = jnp.concatenate([w_own, w_other], axis=0)
        for j in range(8):
            a = pn[0, pl.ds(j, 128, stride=8), :].T
            b = pn[1, pl.ds(j, 128, stride=8), :].T
            v = jnp.concatenate([a, jnp.where(first, b[0:64], b[64:128])], axis=0)
            v = (v * out_gain + out_shift).astype(BF)
            u = jnp.dot(v, w, preferred_element_type=F32) * gate[t * 8 + j]
            ostage[pl.ds(j, 192, stride=8), :] = u
        obf[:, :, pl.ds(t * 8, 8), :] = ostage[...].reshape(24, 8, 8, 128).astype(BF)
        for u in range(3):
            out_copy(t, u).start()
        return carry

    lax.fori_loop(0, 3, finish, 0)

    for t in range(3):
        for u in range(3):
            out_copy(t, u).wait()
            peer_copy(t, u).wait_send()
        to_peer(t, 0).wait_send()
        to_peer(t, 1).wait_send()
    for sem, buf in ((l_send, lsend), (r_send, rsend), (p_send, recv_p)):
        pltpu.make_async_copy(buf.at[pl.ds(0, 189)], buf.at[pl.ds(0, 189)], sem).wait()


def per_device(pair_input, in_gain, in_shift, w_proj, w_gate, out_gain, out_shift, w_out):
    vmem = pl.BlockSpec(memory_space=pltpu.VMEM)
    anyspace = pl.BlockSpec(memory_space=pl.ANY)
    dma = pltpu.SemaphoreType.DMA
    out = pl.pallas_call(
        kernel,
        out_shape=jax.ShapeDtypeStruct((8, 3, 8, 24, 128), BF),
        in_specs=[anyspace] + [vmem] * 7,
        out_specs=anyspace,
        scratch_shapes=[
            pltpu.VMEM((3, 48, 8, 8, 128), BF),
            pltpu.VMEM((9216, 128), F32),
            pltpu.VMEM((256, 128), BF),
            pltpu.VMEM((192, 8, 384), BF),
            pltpu.VMEM((192, 8, 384), BF),
            pltpu.VMEM((3, 512, 128), F32),
            pltpu.VMEM((96, 8, 768), BF),
            pltpu.VMEM((96, 8, 768), BF),
            pltpu.VMEM((96, 8, 768), BF),
            pltpu.VMEM((192, 8, 384), BF),
            pltpu.VMEM((192, 8, 256), BF),
            pltpu.VMEM((24, 192, 128), F32),
            pltpu.VMEM((2, 1024, 128), F32),
            pltpu.VMEM((1536, 128), F32),
            pltpu.VMEM((24, 8, 24, 128), BF),
            dma((3,)),
            dma,
            dma((3,)),
            dma,
            dma,
            dma,
            dma((3,)),
            dma,
            dma((3,)),
            dma,
            dma((3,)),
            dma,
        ],
        compiler_params=pltpu.CompilerParams(
            collective_id=0, has_side_effects=True, vmem_limit_bytes=56 * 2**20
        ),
        name="triangle",
    )(
        pair_input.reshape(8, 3, 8, 24, 128),
        in_gain.reshape(1, 128),
        in_shift.reshape(1, 128),
        w_proj,
        w_gate,
        out_gain.reshape(1, 128),
        out_shift.reshape(1, 128),
        w_out,
    )
    return out.reshape(192, 24, 128)


def solution(mesh):
    placed = (P("row", ("col", "depth"), None), P(), P(), P(), P(), P(), P(), P())
    return jax.shard_map(
        per_device,
        mesh=mesh,
        in_specs=placed,
        out_specs=P("row", ("col", "depth"), None),
        check_vma=False,
    )
```

time: 128 us -> 65.6 us (0.51)
  Pallas kernels: 0 us -> 63 us
  waiting for transfers between devices: 55.5 us -> 0 us
  local copies, waits for them, and re-layouts: 29.1 us -> 2.49 us
  starting transfers between devices: 22.9 us -> 0 us
  matrix products: 12 us -> 0 us
  other arithmetic: 7.58 us -> 0 us
    pallas_call x0 -> x1, Pallas kernels: none -> 63 us  [per_device(): pl.pallas_call(kernel, out_shape=jax.ShapeDtypeStruct((8, 3, 8, 24, 128),...]
    all_to_all x3 -> x0, waiting for transfers between devices: 55.5 us -> none  [joined_exchange(): parts = lax.all_to_all(parts, axis, split_axis=0, concat_axis=0, tiled=True)]
    all_to_all x3 -> x0, starting transfers between devices: 22.9 us -> none  [joined_exchange(): parts = lax.all_to_all(parts, axis, split_axis=0, concat_axis=0, tiled=True)]
    dot_general x4 -> x0, matrix products: 12 us -> none  [the longest x1 3.78 us: per_device(): jnp.einsum('kic,kjc->ijc', left_all, right_all, preferred_element_type=jn...]
    reshape x6 -> x0, local copies, waits for them, and re-layouts: 11.9 us -> none  [the longest x2 6.26 us: in_order(): parts.reshape(*dims[:dim], dims[dim] * dims[dim + 1], *dims[dim + 2:])]
    convert_element_type x4 -> x0, local copies, waits for them, and re-layouts: 6.96 us -> none  [the longest x1 2.88 us: gated_sides(): left_side = (jax.nn.sigmoid(projected[..., :channels]) * projected[..., c...]
    transpose x3 -> x0, local copies, waits for them, and re-layouts: 5.01 us -> none  [the longest x2 4.99 us: in_order(): parts = jnp.moveaxis(parts, 0, dim)]
    another operation x2 -> x0, local copies, waits for them, and re-layouts: 4.83 us -> none  [cut_along(): return jnp.moveaxis(array.reshape(*before, length, -1, *after), dim, 0)]
  transfers between devices with their start and end apart: 3 -> 0, of which waited for: 3 -> 0; matrix products, arithmetic and copies ran while one was open for 13% -> 0% of each run, Pallas kernels for 0% -> 0%
where the time goes in v1:
time: 65.6 us; the launch traced here: 65.5 us
  Pallas kernels  63 us (96%)
  local copies, waits for them, and re-layouts  2.49 us (4%)
    pallas_call x1, Pallas kernels, per_device(): pl.pallas_call(kernel, out_shape=jax.ShapeDtypeStruct((8, 3, 8, 24, 128),...  63 us
    unnamed x1, local copies, waits for them, and re-layouts  2.49 us

profile of v1, /device:TPU:1, one launch (start us, length us, event | category | flops | bytes accessed | tf_op | source)
XLA Modules:
  0.0 65.5 jit_solution(15791574894577565372)
XLA Ops:
  0.0 63.0 %triangle.1 = bf16[8,3,8,24,128]{4,3,2,1,0:T(8,128)(2,1)} custom-call(bf16[8,3,8,24,128]{4,3,2,1,0:T(8,128)(2,1)} %bitcast.7, f32[1,128]{1,0:T(1,128)} %bitcast.8, f32[1,128]{1,0:T(1,128)} %bitcast.9, bf16[128,512]{1,0:T(8,128)(2,1)} %wp_ref.1, bf16[128,128]{1,0:T(8,128)(2,1)} %wg_ref.1, f32[1,128]{1,0:T(1,128)} %bitcast.10, f32[1,128]{1,0:T(1,128)} %bitcast.11, ...), custom_call_target="tpu_custom_call" | custom-call | tf_op jit(solution)/shard_map/triangle/pallas_call | solution.py:287
  63.0 2.5 %copy.10 = bf16[192,24,128]{2,1,0:T(8,128)(2,1)} copy(bf16[192,24,128]{2,1,0:T(8,128)(2,1)} %bitcast.6) | data formatting | bytes 2359296

commit v2 on v1

--- a/solution.py
+++ b/solution.py
@@ -1,4 +1,4 @@
-import functools
+import itertools
 
 import jax
 import jax.numpy as jnp
@@ -24,11 +24,19 @@
     return lax.dot_general(a, b, (((1,), (1,)), ((), ())), preferred_element_type=F32)
 
 
+def hops(step):
+    dzh, dzl, dx, dy = step
+    return (2 if dzh else 0) + dzl + min(dx, 4 - dx) + min(dy, 4 - dy)
+
+
+ORDER = [(1, 0, 2, 2), (0, 1, 2, 2), (0, 1, 0, 0), (1, 1, 2, 2), (1, 1, 0, 0), (1, 0, 1, 2), (0, 0, 3, 0), (1, 0, 2, 1), (0, 0, 0, 3), (1, 0, 2, 3), (0, 0, 0, 1), (1, 0, 3, 2), (0, 0, 1, 0), (0, 1, 1, 2), (0, 1, 3, 0), (0, 1, 2, 1), (0, 1, 0, 3), (0, 1, 2, 3), (0, 1, 0, 1), (0, 1, 3, 2), (0, 1, 1, 0), (1, 1, 1, 2), (1, 1, 3, 0), (1, 1, 2, 1), (1, 1, 0, 3), (1, 1, 2, 3), (1, 1, 0, 1), (1, 1, 3, 2), (1, 1, 1, 0), (0, 1, 0, 2), (0, 1, 2, 0), (0, 1, 1, 1), (0, 1, 3, 3), (0, 1, 1, 3), (0, 1, 3, 1), (1, 1, 0, 2), (1, 1, 2, 0), (1, 1, 1, 1), (1, 1, 3, 3), (1, 1, 1, 3), (1, 1, 3, 1), (0, 0, 2, 2), (1, 0, 0, 0), (1, 0, 0, 2), (0, 0, 2, 0), (1, 0, 1, 1), (0, 0, 3, 3), (1, 0, 1, 3), (0, 0, 3, 1), (1, 0, 2, 0), (0, 0, 0, 2), (1, 0, 3, 1), (0, 0, 1, 3), (1, 0, 3, 3), (0, 0, 1, 1), (0, 0, 1, 2), (1, 0, 3, 0), (0, 0, 2, 1), (1, 0, 0, 3), (0, 0, 2, 3), (1, 0, 0, 1), (0, 0, 3, 2), (1, 0, 1, 0)]
+
+
 def kernel(
     x_ref, ig_ref, is_ref, wp_ref, wg_ref, og_ref, os_ref, wo_ref, out_ref,
     xin, xs, wsel, lsend, rsend, stage, recv_l, recv_r, psend, recv_p, peer_p,
-    gate, pn, ostage, obf,
-    own_sem, x_send, x_recv, l_send, l_recv, r_send, r_recv, p_send, p_recv, e_send, e_recv, o_sem,
+    gate, pn, ostage, wp, wg, wo, vecs,
+    w_sem, own_sem, x_send, x_recv, l_send, l_recv, r_send, r_recv, p_send, p_recv, e_send, e_recv,
 ):
     row = lax.axis_index("row")
     col = lax.axis_index("col")
@@ -40,14 +48,24 @@
     other = {"row": zh * 2 + 1 - core, "col": col, "depth": y}
     low = pl.multiple_of(zh * 384, 128)
 
-    def chip(o):
-        zh2 = rem(zh + div(o, 32), 2)
-        zl2 = rem(zl + div(o, 16), 2)
-        x2 = rem(x + div(o, 4), 4)
-        y2 = rem(y + o, 4)
-        col2 = zl2 * 4 + x2
-        q2 = col2 * 4 + y2
-        return zh2, q2, zh2 * 32 + q2, {"row": zh2 * 2 + core, "col": col2, "depth": y2}
+    rows2 = [(zh, row), (1 - zh, (1 - zh) * 2 + core)]
+    xs2 = [rem(x + d, 4) for d in range(4)]
+    cols2 = [[a * 4 + b for b in xs2] for a in (zl, 1 - zl)]
+    ys2 = [rem(y + d, 4) for d in range(4)]
+
+    def each_chip(use):
+        for dzh, dzl, dx, dy in ORDER:
+            zh2, row2 = rows2[dzh]
+            q2 = cols2[dzl][dx] * 4 + ys2[dy]
+            use(zh2, q2, zh2 * 32 + q2, {"row": row2, "col": cols2[dzl][dx], "depth": ys2[dy]})
+
+    weights = [
+        pltpu.make_async_copy(src, dst, w_sem.at[n])
+        for n, (src, dst) in enumerate(
+            ((wp_ref, wp), (ig_ref, vecs.at[0]), (is_ref, vecs.at[1]), (wg_ref, wg), (og_ref, vecs.at[2]),
+             (os_ref, vecs.at[3]), (wo_ref, wo))
+        )
+    ]
 
     def own_copy(t, u):
         start = core * 128 + u * 64 if u < 2 else 256 + core * 64
@@ -58,50 +76,66 @@
     for t in range(3):
         for u in range(3):
             own_copy(t, u).start()
+    for copy in weights:
+        copy.start()
 
     barrier = pltpu.get_barrier_semaphore()
+    each_chip(lambda zh2, q2, n, device: pl.semaphore_signal(barrier, inc=1, device_id=device))
     pl.semaphore_signal(barrier, inc=1, device_id=other)
 
-    def greet(o, carry):
-        pl.semaphore_signal(barrier, inc=1, device_id=chip(o)[3])
-        return carry
-
-    lax.fori_loop(1, 64, greet, 0)
-
+    for copy in weights:
+        copy.wait()
     for part in range(4):
-        block = wp_ref[:, part * 128 : (part + 1) * 128].astype(F32).T
+        block = wp[:, part * 128 : (part + 1) * 128].astype(F32).T
         stage[0, 0:128, :] = block
         wsel[part * 64 : (part + 1) * 64, :] = stage[0, pl.ds(pl.multiple_of(core * 64, 64), 64), :].astype(BF)
 
+    in_gain = vecs[0]
+    in_shift = vecs[1]
+    mean_of = jnp.full((128, 128), 1.0 / 128.0, BF)
+    mean_of_two = jnp.full((256, 128), 1.0 / 128.0, BF)
+
+    def norm_own(t, carry):
+        pltpu.make_async_copy(xin.at[t, pl.ds(0, 24)], xin.at[t, pl.ds(0, 24)], own_sem.at[t]).wait()
+        for n in range(6):
+            start = core * 16 + n * 4 if n < 4 else 32 + core * 8 + (n - 4) * 4
+            raw = xin[t, pl.ds(start, 4)].reshape(256, 128)
+            v = raw.astype(F32) - jnp.dot(raw, mean_of, preferred_element_type=F32)
+            square = v * v
+            upper = square.astype(BF)
+            lower = (square - upper.astype(F32)).astype(BF)
+            variance = jnp.dot(
+                jnp.concatenate([upper, lower], axis=1), mean_of_two, preferred_element_type=F32
+            )
+            v = v * lax.rsqrt(variance + EPS) * in_gain + in_shift
+            xs[pl.ds(pl.multiple_of(t * 3072 + start * 64, 256), 256), :] = v
+            xin[t, pl.ds(start, 4)] = v.astype(BF).reshape(4, 8, 8, 128)
+        return carry
+
+    lax.fori_loop(0, 3, norm_own, 0)
+
     pl.semaphore_wait(barrier, 64)
 
     def peer_copy(t, u):
-        start = core * 128 + u * 64 if u < 2 else 256 + core * 64
+        here = pl.ds(core * 16, 16) if u == 0 else pl.ds(32 + core * 8, 8)
         return pltpu.make_async_remote_copy(
-            src_ref=x_ref.at[:, u, :, pl.ds(t * 8, 8), :],
-            dst_ref=xin.at[t, pl.ds(div(start, 8), 8)],
+            src_ref=xin.at[t, here],
+            dst_ref=xin.at[t, here],
             send_sem=x_send,
             recv_sem=x_recv.at[t],
             device_id=other,
         )
 
     for t in range(3):
-        for u in range(3):
+        for u in range(2):
             peer_copy(t, u).start()
 
-    in_gain = ig_ref[...]
-    in_shift = is_ref[...]
-
-    def norm_rows(t):
-        def chunk(i, carry):
-            v = xin[t, pl.ds(i * 4, 4)].astype(F32)
-            v = v - jnp.mean(v, axis=-1, keepdims=True)
-            v = v * lax.rsqrt(jnp.mean(v * v, axis=-1, keepdims=True) + EPS)
-            v = v * in_gain.reshape(1, 1, 1, 128) + in_shift.reshape(1, 1, 1, 128)
-            xs[pl.ds(pl.multiple_of(t * 3072 + i * 256, 256), 256), :] = v.reshape(256, 128)
-            return carry
-
-        lax.fori_loop(0, 12, chunk, 0)
+    def widen_peer(t):
+        for n in range(6):
+            start = (1 - core) * 16 + n * 4 if n < 4 else 32 + (1 - core) * 8 + (n - 4) * 4
+            xs[pl.ds(pl.multiple_of(t * 3072 + start * 64, 256), 256), :] = (
+                xin[t, pl.ds(start, 4)].reshape(256, 128).astype(F32)
+            )
 
     def project(t, base, dst):
         w = wsel[base : base + 128, :]
@@ -115,15 +149,13 @@
             dst[pl.ds(t * 64, 64), :, c * 128 : (c + 1) * 128] = stage[c].reshape(64, 8, 128).astype(BF)
 
     def left(t, carry):
-        pltpu.make_async_copy(xin.at[t, pl.ds(0, 24)], xin.at[t, pl.ds(0, 24)], own_sem.at[t]).wait()
         pltpu.make_async_copy(xin.at[t, pl.ds(0, 24)], xin.at[t, pl.ds(0, 24)], x_recv.at[t]).wait()
-        norm_rows(t)
+        widen_peer(t)
         project(t, 0, lsend)
         late = div(t, 2)
         group = div(q, 16) * 48 + rem(div(q, 8), 2) * (16 - 8 * late) + t * 8 * (1 - late) + 32 * late + rem(q, 8)
 
-        def send(o, carry):
-            _, _, n, device = chip(o)
+        def send(zh2, q2, n, device):
             pltpu.make_async_remote_copy(
                 src_ref=lsend.at[t * 64 + n],
                 dst_ref=recv_l.at[group, :, pl.ds(low, 384)],
@@ -131,9 +163,8 @@
                 recv_sem=l_recv,
                 device_id=device,
             ).start()
-            return carry
-
-        lax.fori_loop(1, 64, send, 0)
+
+        each_chip(send)
         recv_l[group, :, pl.ds(low, 384)] = lsend[t * 64 + me]
         return carry
 
@@ -142,8 +173,7 @@
     def right(t, carry):
         project(t, 128, rsend)
 
-        def send(o, carry):
-            _, _, n, device = chip(o)
+        def send(zh2, q2, n, device):
             pltpu.make_async_remote_copy(
                 src_ref=rsend.at[t * 64 + n],
                 dst_ref=recv_r.at[t * 32 + q, :, pl.ds(low, 384)],
@@ -151,16 +181,15 @@
                 recv_sem=r_recv.at[t],
                 device_id=device,
             ).start()
-            return carry
-
-        lax.fori_loop(1, 64, send, 0)
+
+        each_chip(send)
         recv_r[t * 32 + q, :, pl.ds(low, 384)] = rsend[t * 64 + me]
         return carry
 
     lax.fori_loop(0, 3, right, 0)
 
     def gates(t, carry):
-        w = wg_ref[...]
+        w = wg[...]
         for i in range(8):
             a = xs[pl.ds(t * 3072 + core * 1024 + i, 128, stride=8), :].astype(BF)
             b = xs[pl.ds(t * 3072 + 2048 + core * 512 + i, 64, stride=8), :].astype(BF)
@@ -181,8 +210,7 @@
                 dot_nt(rows, cols).astype(BF).reshape(32, 8, 256)
             )
 
-        def send(o, carry):
-            zh2, q2, _, device = chip(o)
+        def send(zh2, q2, n, device):
             pltpu.make_async_remote_copy(
                 src_ref=psend.at[t * 32 + q2, :, pl.ds(pl.multiple_of(zh2 * 384, 128), 384)],
                 dst_ref=recv_p.at[t * 64 + me],
@@ -190,9 +218,8 @@
                 recv_sem=p_recv.at[t],
                 device_id=device,
             ).start()
-            return carry
-
-        lax.fori_loop(1, 64, send, 0)
+
+        each_chip(send)
         recv_p[t * 64 + me] = psend[t * 32 + q, :, pl.ds(low, 384)]
         return carry
 
@@ -210,13 +237,8 @@
 
     own_lane = pl.multiple_of(core * 128, 128)
     first = core == 0
-    out_gain = jnp.where(first, og_ref[...], pltpu.roll(og_ref[...], 64, 1))
-    out_shift = jnp.where(first, os_ref[...], pltpu.roll(os_ref[...], 64, 1))
-
-    def out_copy(t, u):
-        return pltpu.make_async_copy(
-            obf.at[pl.ds(u * 8, 8), :, pl.ds(t * 8, 8), :], out_ref.at[:, u, :, pl.ds(t * 8, 8), :], o_sem
-        )
+    out_gain = jnp.where(first, vecs[2], pltpu.roll(vecs[2], 64, 1))
+    out_shift = jnp.where(first, vecs[3], pltpu.roll(vecs[3], 64, 1))
 
     def finish(t, carry):
         pltpu.make_async_copy(rsend.at[pl.ds(0, 63)], rsend.at[pl.ds(0, 63)], p_recv.at[t]).wait()
@@ -253,8 +275,8 @@
             for c in range(2):
                 pn[c, lo * 8 : lo * 8 + 128, :] = a[:, c * 128 : (c + 1) * 128]
                 pn[c, 512 + lo * 8 : 512 + lo * 8 + 128, :] = b[:, c * 128 : (c + 1) * 128]
-        w_own = wo_ref[pl.ds(pl.multiple_of(core * 64, 64), 64), :]
-        w_other = wo_ref[pl.ds(pl.multiple_of((1 - core) * 64, 64), 64), :]
+        w_own = wo[pl.ds(pl.multiple_of(core * 64, 64), 64), :]
+        w_other = wo[pl.ds(pl.multiple_of((1 - core) * 64, 64), 64), :]
         w = jnp.concatenate([w_own, w_other], axis=0)
         for j in range(8):
             a = pn[0, pl.ds(j, 128, stride=8), :].T
@@ -263,16 +285,16 @@
             v = (v * out_gain + out_shift).astype(BF)
             u = jnp.dot(v, w, preferred_element_type=F32) * gate[t * 8 + j]
             ostage[pl.ds(j, 192, stride=8), :] = u
-        obf[:, :, pl.ds(t * 8, 8), :] = ostage[...].reshape(24, 8, 8, 128).astype(BF)
         for u in range(3):
-            out_copy(t, u).start()
+            out_ref[:, u, :, pl.ds(pl.multiple_of(t * 8, 8), 8), :] = (
+                ostage[u * 512 : (u + 1) * 512, :].reshape(8, 8, 8, 128).astype(BF)
+            )
         return carry
 
     lax.fori_loop(0, 3, finish, 0)
 
     for t in range(3):
-        for u in range(3):
-            out_copy(t, u).wait()
+        for u in range(2):
             peer_copy(t, u).wait_send()
         to_peer(t, 0).wait_send()
         to_peer(t, 1).wait_send()
@@ -282,13 +304,13 @@
 
 def per_device(pair_input, in_gain, in_shift, w_proj, w_gate, out_gain, out_shift, w_out):
     vmem = pl.BlockSpec(memory_space=pltpu.VMEM)
-    anyspace = pl.BlockSpec(memory_space=pl.ANY)
+    anyspace = pl.BlockSpec(memory_space=pltpu.HBM)
     dma = pltpu.SemaphoreType.DMA
     out = pl.pallas_call(
         kernel,
-        out_shape=jax.ShapeDtypeStruct((8, 3, 8, 24, 128), BF),
-        in_specs=[anyspace] + [vmem] * 7,
-        out_specs=anyspace,
+        out_shape=pltpu.VMEM((8, 3, 8, 24, 128), BF),
+        in_specs=[anyspace] * 8,
+        out_specs=vmem,
         scratch_shapes=[
             pltpu.VMEM((3, 48, 8, 8, 128), BF),
             pltpu.VMEM((9216, 128), F32),
@@ -304,33 +326,41 @@
             pltpu.VMEM((24, 192, 128), F32),
             pltpu.VMEM((2, 1024, 128), F32),
             pltpu.VMEM((1536, 128), F32),
-            pltpu.VMEM((24, 8, 24, 128), BF),
-            dma((3,)),
-            dma,
-            dma((3,)),
-            dma,
-            dma,
-            dma,
-            dma((3,)),
-            dma,
-            dma((3,)),
-            dma,
-            dma((3,)),
-            dma,
+            pltpu.VMEM((128, 512), BF),
+            pltpu.VMEM((128, 128), BF),
+            pltpu.VMEM((128, 128), BF),
+            pltpu.VMEM((4, 1, 128), F32),
+            dma((7,)),
+            dma((3,)),
+            dma,
+            dma((3,)),
+            dma,
+            dma,
+            dma,
+            dma((3,)),
+            dma,
+            dma((3,)),
+            dma,
+            dma((3,)),
         ],
         compiler_params=pltpu.CompilerParams(
-            collective_id=0, has_side_effects=True, vmem_limit_bytes=56 * 2**20
+            collective_id=0, has_side_effects=True, vmem_limit_bytes=int(54 * 2**20)
         ),
         name="triangle",
     )(
-        pair_input.reshape(8, 3, 8, 24, 128),
-        in_gain.reshape(1, 128),
-        in_shift.reshape(1, 128),
-        w_proj,
-        w_gate,
-        out_gain.reshape(1, 128),
-        out_shift.reshape(1, 128),
-        w_out,
+        *(
+            pltpu.with_memory_space_constraint(a, pltpu.HBM)
+            for a in (
+                pair_input.reshape(8, 3, 8, 24, 128),
+                in_gain.reshape(1, 128),
+                in_shift.reshape(1, 128),
+                w_proj,
+                w_gate,
+                out_gain.reshape(1, 128),
+                out_shift.reshape(1, 128),
+                w_out,
+            )
+        )
     )
     return out.reshape(192, 24, 128)
 

time: 65.6 us -> 57.5 us (0.88)
  Pallas kernels: 63 us -> 56.3 us
  local copies, waits for them, and re-layouts: 2.49 us -> 1.02 us
    pallas_call x1, Pallas kernels: 63 us -> 56.3 us  [per_device(): pl.pallas_call(kernel, out_shape=pltpu.VMEM((8, 3, 8, 24, 128), BF), in_s...]
    unnamed x1, local copies, waits for them, and re-layouts: 2.49 us -> 1.02 us
where the time goes in v2:
time: 57.5 us; the launch traced here: 57.4 us
  Pallas kernels  56.3 us (98%)
  local copies, waits for them, and re-layouts  1.02 us (2%)
    pallas_call x1, Pallas kernels, per_device(): pl.pallas_call(kernel, out_shape=pltpu.VMEM((8, 3, 8, 24, 128), BF), in_s...  56.3 us

profile of v2, /device:TPU:1, one launch (start us, length us, event | category | flops | bytes accessed | tf_op | source)
XLA Modules:
  0.0 57.4 jit_solution(9328114969741697046)
XLA Ops:
  0.0 56.3 %triangle.1 = bf16[8,3,8,24,128]{4,3,2,1,0:T(8,128)(2,1)S(1)} custom-call(bf16[8,3,8,24,128]{4,3,2,1,0:T(8,128)(2,1)} %bitcast.7, f32[1,128]{1,0:T(1,128)} %bitcast.8, f32[1,128]{1,0:T(1,128)} %bitcast.9, bf16[128,512]{1,0:T(8,128)(2,1)} %wp_ref.1, bf16[128,128]{1,0:T(8,128)(2,1)} %wg_ref.1, f32[1,128]{1,0:T(1,128)} %bitcast.10, f32[1,128]{1,0:T(1,128)} %bitcast.11, ...), custom_call_target="tpu_custom_call" | custom-call | tf_op jit(solution)/shard_map/triangle/pallas_call | solution.py:309
  56.3 1.0 %copy.10 = bf16[192,24,128]{2,1,0:T(8,128)(2,1)} copy(bf16[192,24,128]{2,1,0:T(8,128)(2,1)S(1)} %bitcast.6) | data formatting | bytes 2359296

commit v3 on v2

--- a/solution.py
+++ b/solution.py
@@ -32,9 +32,12 @@
 ORDER = [(1, 0, 2, 2), (0, 1, 2, 2), (0, 1, 0, 0), (1, 1, 2, 2), (1, 1, 0, 0), (1, 0, 1, 2), (0, 0, 3, 0), (1, 0, 2, 1), (0, 0, 0, 3), (1, 0, 2, 3), (0, 0, 0, 1), (1, 0, 3, 2), (0, 0, 1, 0), (0, 1, 1, 2), (0, 1, 3, 0), (0, 1, 2, 1), (0, 1, 0, 3), (0, 1, 2, 3), (0, 1, 0, 1), (0, 1, 3, 2), (0, 1, 1, 0), (1, 1, 1, 2), (1, 1, 3, 0), (1, 1, 2, 1), (1, 1, 0, 3), (1, 1, 2, 3), (1, 1, 0, 1), (1, 1, 3, 2), (1, 1, 1, 0), (0, 1, 0, 2), (0, 1, 2, 0), (0, 1, 1, 1), (0, 1, 3, 3), (0, 1, 1, 3), (0, 1, 3, 1), (1, 1, 0, 2), (1, 1, 2, 0), (1, 1, 1, 1), (1, 1, 3, 3), (1, 1, 1, 3), (1, 1, 3, 1), (0, 0, 2, 2), (1, 0, 0, 0), (1, 0, 0, 2), (0, 0, 2, 0), (1, 0, 1, 1), (0, 0, 3, 3), (1, 0, 1, 3), (0, 0, 3, 1), (1, 0, 2, 0), (0, 0, 0, 2), (1, 0, 3, 1), (0, 0, 1, 3), (1, 0, 3, 3), (0, 0, 1, 1), (0, 0, 1, 2), (1, 0, 3, 0), (0, 0, 2, 1), (1, 0, 0, 3), (0, 0, 2, 3), (1, 0, 0, 1), (0, 0, 3, 2), (1, 0, 1, 0)]
 
 
+FAR = sorted(ORDER, key=lambda s: -hops(s))
+
+
 def kernel(
     x_ref, ig_ref, is_ref, wp_ref, wg_ref, og_ref, os_ref, wo_ref, out_ref,
-    xin, xs, wsel, lsend, rsend, stage, recv_l, recv_r, psend, recv_p, peer_p,
+    xin, xs, wall, lown, lsend, rsend, stage, recv_l, recv_r, psend, recv_p, peer_p,
     gate, pn, ostage, wp, wg, wo, vecs,
     w_sem, own_sem, x_send, x_recv, l_send, l_recv, r_send, r_recv, p_send, p_recv, e_send, e_recv,
 ):
@@ -48,16 +51,24 @@
     other = {"row": zh * 2 + 1 - core, "col": col, "depth": y}
     low = pl.multiple_of(zh * 384, 128)
 
-    rows2 = [(zh, row), (1 - zh, (1 - zh) * 2 + core)]
+    rows2 = [(zh, row, zh * 2 + 1 - core), (1 - zh, (1 - zh) * 2 + core, (1 - zh) * 2 + 1 - core)]
     xs2 = [rem(x + d, 4) for d in range(4)]
     cols2 = [[a * 4 + b for b in xs2] for a in (zl, 1 - zl)]
     ys2 = [rem(y + d, 4) for d in range(4)]
 
-    def each_chip(use):
-        for dzh, dzl, dx, dy in ORDER:
-            zh2, row2 = rows2[dzh]
+    def each_chip(use, order=ORDER):
+        for dzh, dzl, dx, dy in order:
+            zh2, row2, _ = rows2[dzh]
             q2 = cols2[dzl][dx] * 4 + ys2[dy]
             use(zh2, q2, zh2 * 32 + q2, {"row": row2, "col": cols2[dzl][dx], "depth": ys2[dy]})
+
+    def each_device(use, order):
+        for dzh, dzl, dx, dy in order:
+            zh2, row2, cross2 = rows2[dzh]
+            n = zh2 * 32 + cols2[dzl][dx] * 4 + ys2[dy]
+            use(n, core, {"row": row2, "col": cols2[dzl][dx], "depth": ys2[dy]})
+            use(n, 1 - core, {"row": cross2, "col": cols2[dzl][dx], "depth": ys2[dy]})
+        use(me, 1 - core, other)
 
     weights = [
         pltpu.make_async_copy(src, dst, w_sem.at[n])
@@ -80,15 +91,12 @@
         copy.start()
 
     barrier = pltpu.get_barrier_semaphore()
-    each_chip(lambda zh2, q2, n, device: pl.semaphore_signal(barrier, inc=1, device_id=device))
-    pl.semaphore_signal(barrier, inc=1, device_id=other)
+    each_device(lambda n, owner, device: pl.semaphore_signal(barrier, inc=1, device_id=device), FAR)
 
     for copy in weights:
         copy.wait()
     for part in range(4):
-        block = wp[:, part * 128 : (part + 1) * 128].astype(F32).T
-        stage[0, 0:128, :] = block
-        wsel[part * 64 : (part + 1) * 64, :] = stage[0, pl.ds(pl.multiple_of(core * 64, 64), 64), :].astype(BF)
+        wall[part * 128 : (part + 1) * 128, :] = wp[:, part * 128 : (part + 1) * 128].astype(F32).T.astype(BF)
 
     in_gain = vecs[0]
     in_shift = vecs[1]
@@ -112,9 +120,19 @@
             xin[t, pl.ds(start, 4)] = v.astype(BF).reshape(4, 8, 8, 128)
         return carry
 
-    lax.fori_loop(0, 3, norm_own, 0)
-
-    pl.semaphore_wait(barrier, 64)
+    def group_of(t):
+        late = div(t, 2)
+        return div(q, 16) * 48 + rem(div(q, 8), 2) * (16 - 8 * late) + t * 8 * (1 - late) + 32 * late + rem(q, 8)
+
+    norm_own(0, 0)
+    for i in range(8):
+        rows = xs[pl.ds(core * 1024 + i, 128, stride=8), :].astype(BF)
+        p = dot_nt(wall[0:256, :], rows)
+        pn[0, pl.ds(i, 128, stride=8), :] = jax.nn.sigmoid(p[0:128]) * p[128:256]
+    lown[...] = pn[0].reshape(128, 8, 128).astype(BF)
+    lax.fori_loop(1, 3, norm_own, 0)
+
+    pl.semaphore_wait(barrier, 127)
 
     def peer_copy(t, u):
         here = pl.ds(core * 16, 16) if u == 0 else pl.ds(32 + core * 8, 8)
@@ -130,6 +148,21 @@
         for u in range(2):
             peer_copy(t, u).start()
 
+    own_tile = pl.ds(pl.multiple_of(zh * 384 + core * 128, 128), 128)
+    group = group_of(jnp.int32(0))
+
+    def send_own(n, owner, device):
+        pltpu.make_async_remote_copy(
+            src_ref=lown.at[owner * 64 + n],
+            dst_ref=recv_l.at[group, :, own_tile],
+            send_sem=l_send,
+            recv_sem=l_recv,
+            device_id=device,
+        ).start()
+
+    each_device(send_own, ORDER)
+    recv_l[group, :, own_tile] = lown[core * 64 + me]
+
     def widen_peer(t):
         for n in range(6):
             start = (1 - core) * 16 + n * 4 if n < 4 else 32 + (1 - core) * 8 + (n - 4) * 4
@@ -137,41 +170,50 @@
                 xin[t, pl.ds(start, 4)].reshape(256, 128).astype(F32)
             )
 
-    def project(t, base, dst):
-        w = wsel[base : base + 128, :]
+    def project(t, base, dst, tiles):
+        w = jnp.concatenate(
+            [wall[pl.ds(pl.multiple_of(part * 128 + core * 64, 64), 64), :] for part in (base, base + 1)], axis=0
+        )
         for i in range(8):
-            rows = xs[pl.ds(t * 3072 + i, 384, stride=8), :].astype(BF)
+            rows = xs[pl.ds(t * 3072 + tiles[0] * 1024 + i, len(tiles) * 128, stride=8), :].astype(BF)
             p = dot_nt(w, rows)
             side = jax.nn.sigmoid(p[0:64]) * p[64:128]
-            for c in range(3):
-                stage[c, pl.ds(i, 64, stride=8), :] = side[:, c * 128 : (c + 1) * 128]
-        for c in range(3):
+            for n, c in enumerate(tiles):
+                stage[c, pl.ds(i, 64, stride=8), :] = side[:, n * 128 : (n + 1) * 128]
+        for c in tiles:
             dst[pl.ds(t * 64, 64), :, c * 128 : (c + 1) * 128] = stage[c].reshape(64, 8, 128).astype(BF)
 
-    def left(t, carry):
+    def left(t, tiles):
         pltpu.make_async_copy(xin.at[t, pl.ds(0, 24)], xin.at[t, pl.ds(0, 24)], x_recv.at[t]).wait()
         widen_peer(t)
-        project(t, 0, lsend)
-        late = div(t, 2)
-        group = div(q, 16) * 48 + rem(div(q, 8), 2) * (16 - 8 * late) + t * 8 * (1 - late) + 32 * late + rem(q, 8)
+        project(t, 0, lsend, tiles)
+        group = group_of(t)
+        size = len(tiles) * 128
+        src_lanes = pl.ds(tiles[0] * 128, size)
+        dst_lanes = pl.ds(pl.multiple_of(low + tiles[0] * 128, 128), size)
 
         def send(zh2, q2, n, device):
             pltpu.make_async_remote_copy(
-                src_ref=lsend.at[t * 64 + n],
-                dst_ref=recv_l.at[group, :, pl.ds(low, 384)],
+                src_ref=lsend.at[t * 64 + n, :, src_lanes],
+                dst_ref=recv_l.at[group, :, dst_lanes],
                 send_sem=l_send,
                 recv_sem=l_recv,
                 device_id=device,
             ).start()
 
         each_chip(send)
-        recv_l[group, :, pl.ds(low, 384)] = lsend[t * 64 + me]
-        return carry
-
-    lax.fori_loop(0, 3, left, 0)
+        recv_l[group, :, dst_lanes] = lsend[t * 64 + me, :, src_lanes]
+
+    left(jnp.int32(0), (2,))
+
+    def left_all(t, carry):
+        left(t, (0, 1, 2))
+        return carry
+
+    lax.fori_loop(1, 3, left_all, 0)
 
     def right(t, carry):
-        project(t, 128, rsend)
+        project(t, 2, rsend, (0, 1, 2))
 
         def send(zh2, q2, n, device):
             pltpu.make_async_remote_copy(
@@ -199,7 +241,7 @@
 
     lax.fori_loop(0, 3, gates, 0)
 
-    pltpu.make_async_copy(lsend.at[pl.ds(0, 189)], lsend.at[pl.ds(0, 189)], l_recv).wait()
+    pltpu.make_async_copy(xs.at[pl.ds(0, 2272)], xs.at[pl.ds(0, 2272)], l_recv).wait()
 
     def product(t, carry):
         pltpu.make_async_copy(rsend.at[pl.ds(0, 63)], rsend.at[pl.ds(0, 63)], r_recv.at[t]).wait()
@@ -298,7 +340,8 @@
             peer_copy(t, u).wait_send()
         to_peer(t, 0).wait_send()
         to_peer(t, 1).wait_send()
-    for sem, buf in ((l_send, lsend), (r_send, rsend), (p_send, recv_p)):
+    pltpu.make_async_copy(xs.at[pl.ds(0, 2272)], xs.at[pl.ds(0, 2272)], l_send).wait()
+    for sem, buf in ((r_send, rsend), (p_send, recv_p)):
         pltpu.make_async_copy(buf.at[pl.ds(0, 189)], buf.at[pl.ds(0, 189)], sem).wait()
 
 
@@ -314,7 +357,8 @@
         scratch_shapes=[
             pltpu.VMEM((3, 48, 8, 8, 128), BF),
             pltpu.VMEM((9216, 128), F32),
-            pltpu.VMEM((256, 128), BF),
+            pltpu.VMEM((512, 128), BF),
+            pltpu.VMEM((128, 8, 128), BF),
             pltpu.VMEM((192, 8, 384), BF),
             pltpu.VMEM((192, 8, 384), BF),
             pltpu.VMEM((3, 512, 128), F32),

time: 57.5 us -> 55.9 us (0.972)
  Pallas kernels: 56.3 us -> 54.8 us
    pallas_call x1, Pallas kernels: 56.3 us -> 54.8 us  [per_device(): pl.pallas_call(kernel, out_shape=pltpu.VMEM((8, 3, 8, 24, 128), BF), in_s...]
where the time goes in v3:
time: 55.9 us; the launch traced here: 55.8 us
  Pallas kernels  54.8 us (98%)
  local copies, waits for them, and re-layouts  1.02 us (2%)
    pallas_call x1, Pallas kernels, per_device(): pl.pallas_call(kernel, out_shape=pltpu.VMEM((8, 3, 8, 24, 128), BF), in_s...  54.8 us

profile of v3, /device:TPU:1, one launch (start us, length us, event | category | flops | bytes accessed | tf_op | source)
XLA Modules:
  0.0 55.8 jit_solution(776511502189288200)
XLA Ops:
  0.0 54.8 %triangle.1 = bf16[8,3,8,24,128]{4,3,2,1,0:T(8,128)(2,1)S(1)} custom-call(bf16[8,3,8,24,128]{4,3,2,1,0:T(8,128)(2,1)} %bitcast.7, f32[1,128]{1,0:T(1,128)} %bitcast.8, f32[1,128]{1,0:T(1,128)} %bitcast.9, bf16[128,512]{1,0:T(8,128)(2,1)} %wp_ref.1, bf16[128,128]{1,0:T(8,128)(2,1)} %wg_ref.1, f32[1,128]{1,0:T(1,128)} %bitcast.10, f32[1,128]{1,0:T(1,128)} %bitcast.11, ...), custom_call_target="tpu_custom_call" | custom-call | tf_op jit(solution)/shard_map/triangle/pallas_call | solution.py:352
  54.8 1.0 %copy.10 = bf16[192,24,128]{2,1,0:T(8,128)(2,1)} copy(bf16[192,24,128]{2,1,0:T(8,128)(2,1)S(1)} %bitcast.6) | data formatting | bytes 2359296

commit v4 on v3

--- a/solution.py
+++ b/solution.py
@@ -37,9 +37,9 @@
 
 def kernel(
     x_ref, ig_ref, is_ref, wp_ref, wg_ref, og_ref, os_ref, wo_ref, out_ref,
-    xin, xs, wall, lown, lsend, rsend, stage, recv_l, recv_r, psend, recv_p, peer_p,
+    xin, xs, wall, lown, lsend, rsend, stage, recv_l, recv_r, psend, recv_p, recv_d, peer_p,
     gate, pn, ostage, wp, wg, wo, vecs,
-    w_sem, own_sem, x_send, x_recv, l_send, l_recv, r_send, r_recv, p_send, p_recv, e_send, e_recv,
+    w_sem, own_sem, x_send, x_recv, l_send, l_recv, r_send, r_recv, p_send, p_recv, d_recv, e_send, e_recv,
 ):
     row = lax.axis_index("row")
     col = lax.axis_index("col")
@@ -130,8 +130,6 @@
         p = dot_nt(wall[0:256, :], rows)
         pn[0, pl.ds(i, 128, stride=8), :] = jax.nn.sigmoid(p[0:128]) * p[128:256]
     lown[...] = pn[0].reshape(128, 8, 128).astype(BF)
-    lax.fori_loop(1, 3, norm_own, 0)
-
     pl.semaphore_wait(barrier, 127)
 
     def peer_copy(t, u):
@@ -144,9 +142,11 @@
             device_id=other,
         )
 
-    for t in range(3):
+    def to_peer_rows(t):
         for u in range(2):
             peer_copy(t, u).start()
+
+    to_peer_rows(0)
 
     own_tile = pl.ds(pl.multiple_of(zh * 384 + core * 128, 128), 128)
     group = group_of(jnp.int32(0))
@@ -204,7 +204,11 @@
         each_chip(send)
         recv_l[group, :, dst_lanes] = lsend[t * 64 + me, :, src_lanes]
 
+    norm_own(1, 0)
+    to_peer_rows(1)
     left(jnp.int32(0), (2,))
+    norm_own(2, 0)
+    to_peer_rows(2)
 
     def left_all(t, carry):
         left(t, (0, 1, 2))
@@ -243,7 +247,7 @@
 
     pltpu.make_async_copy(xs.at[pl.ds(0, 2272)], xs.at[pl.ds(0, 2272)], l_recv).wait()
 
-    def product(t, carry):
+    def product(t):
         pltpu.make_async_copy(rsend.at[pl.ds(0, 63)], rsend.at[pl.ds(0, 63)], r_recv.at[t]).wait()
         rows = recv_r[pl.ds(t * 32, 32)].reshape(256, 768)
         for part in range(3):
@@ -251,6 +255,9 @@
             psend[pl.ds(t * 32, 32), :, part * 256 : (part + 1) * 256] = (
                 dot_nt(rows, cols).astype(BF).reshape(32, 8, 256)
             )
+
+    def product_early(t, carry):
+        product(t)
 
         def send(zh2, q2, n, device):
             pltpu.make_async_remote_copy(
@@ -265,7 +272,35 @@
         recv_p[t * 64 + me] = psend[t * 32 + q, :, pl.ds(low, 384)]
         return carry
 
-    lax.fori_loop(0, 3, product, 0)
+    lax.fori_loop(0, 2, product_early, 0)
+
+    product(jnp.int32(2))
+    shared = pl.ds(pl.multiple_of(low + 256, 128), 128)
+
+    def send_shared(zh2, q2, n, device):
+        pltpu.make_async_remote_copy(
+            src_ref=psend.at[64 + q2, :, pl.ds(pl.multiple_of(zh2 * 384 + 256, 128), 128)],
+            dst_ref=recv_p.at[128 + me, :, pl.ds(256, 128)],
+            send_sem=p_send,
+            recv_sem=p_recv.at[2],
+            device_id=device,
+        ).start()
+
+    each_chip(send_shared)
+    recv_p[128 + me, :, 256:384] = psend[64 + q, :, shared]
+
+    def send_last(n, owner, device):
+        lane = pl.multiple_of(div(n, 32) * 384 + owner * 128, 128)
+        pltpu.make_async_remote_copy(
+            src_ref=psend.at[64 + rem(n, 32), :, pl.ds(lane, 128)],
+            dst_ref=recv_d.at[me if owner is core else 64 + me],
+            send_sem=p_send,
+            recv_sem=d_recv,
+            device_id=device,
+        ).start()
+
+    each_device(send_last, ORDER)
+    recv_d[me] = psend[64 + q, :, own_tile]
 
     def to_peer(t, half):
         lane = pl.multiple_of((1 - core) * 128, 128) if half == 0 else 256
@@ -282,67 +317,82 @@
     out_gain = jnp.where(first, vecs[2], pltpu.roll(vecs[2], 64, 1))
     out_shift = jnp.where(first, vecs[3], pltpu.roll(vecs[3], 64, 1))
 
-    def finish(t, carry):
+    w_out = jnp.concatenate(
+        [wo[pl.ds(pl.multiple_of(half * 64, 64), 64), :] for half in (core, 1 - core)], axis=0
+    )
+
+    def standardize(slot, read):
+        total = jnp.zeros((8, 128), F32)
+        for lo in range(0, 64, 16):
+            a, b = read(lo, 16)
+            total = total + (jnp.sum(a.astype(F32), axis=0) + jnp.sum(b.astype(F32), axis=0))
+        average = (total * (1.0 / 128.0))[None]
+        total = jnp.zeros((8, 128), F32)
+        for lo in range(0, 64, 16):
+            a, b = read(lo, 16)
+            a, b = a.astype(F32) - average, b.astype(F32) - average
+            total = total + (jnp.sum(a * a, axis=0) + jnp.sum(b * b, axis=0))
+        scale = lax.rsqrt(total * (1.0 / 128.0) + EPS)[None]
+        for lo in range(0, 64, 16):
+            a, b = read(lo, 16)
+            pn[slot, lo * 8 : lo * 8 + 128, :] = ((a.astype(F32) - average) * scale).reshape(128, 128)
+            pn[slot, 512 + lo * 8 : 640 + lo * 8, :] = ((b.astype(F32) - average) * scale).reshape(128, 128)
+
+    def project_out(t, slot):
+        rows = 64 if slot else 128
+        for j in range(8):
+            v = pn[slot, pl.ds(j, 128, stride=8), :].T
+            if slot:
+                v = jnp.where(first, v[0:64], v[64:128])
+            v = (v * out_gain + out_shift).astype(BF)
+            u = jnp.dot(v, w_out, preferred_element_type=F32)
+            ostage[pl.ds(slot * 1024 + j, rows, stride=8), :] = u * gate[t * 8 + j, slot * 128 : slot * 128 + rows]
+        for u in ((2,) if slot else (0, 1)):
+            out_ref[:, u, :, pl.ds(pl.multiple_of(t * 8, 8), 8), :] = (
+                ostage[u * 512 : (u + 1) * 512, :].reshape(8, 8, 8, 128).astype(BF)
+            )
+
+    def read_shared(t):
+        return lambda lo, size: (
+            recv_p[pl.ds(t * 64 + lo, size), :, 256:384], peer_p[pl.ds(t * 64 + lo, size), :, 128:256]
+        )
+
+    def finish_early(t, carry):
         pltpu.make_async_copy(rsend.at[pl.ds(0, 63)], rsend.at[pl.ds(0, 63)], p_recv.at[t]).wait()
         to_peer(t, 0).start()
         to_peer(t, 1).start()
-        pltpu.make_async_copy(
-            peer_p.at[pl.ds(0, 64)], peer_p.at[pl.ds(0, 64)], e_recv.at[t]
-        ).wait()
-
-        def parts(lo, size):
-            here = pl.ds(t * 64 + lo, size)
-            return (
-                jnp.concatenate(
-                    [recv_p[here, :, pl.ds(own_lane, 128)], recv_p[here, :, 256:384]], axis=-1
-                ).astype(F32),
-                peer_p[here].astype(F32),
-            )
-
-        total = jnp.zeros((8, 256), F32)
-        for lo in range(0, 64, 16):
-            a, b = parts(lo, 16)
-            total = total + (jnp.sum(a, axis=0) + jnp.sum(b, axis=0))
-        average = total * (1.0 / 128.0)
-        total = jnp.zeros((8, 256), F32)
-        for lo in range(0, 64, 16):
-            a, b = parts(lo, 16)
-            a, b = a - average[None], b - average[None]
-            total = total + (jnp.sum(a * a, axis=0) + jnp.sum(b * b, axis=0))
-        scale = lax.rsqrt(total * (1.0 / 128.0) + EPS)
-        for lo in range(0, 64, 16):
-            a, b = parts(lo, 16)
-            a = ((a - average[None]) * scale[None]).reshape(128, 256)
-            b = ((b - average[None]) * scale[None]).reshape(128, 256)
-            for c in range(2):
-                pn[c, lo * 8 : lo * 8 + 128, :] = a[:, c * 128 : (c + 1) * 128]
-                pn[c, 512 + lo * 8 : 512 + lo * 8 + 128, :] = b[:, c * 128 : (c + 1) * 128]
-        w_own = wo[pl.ds(pl.multiple_of(core * 64, 64), 64), :]
-        w_other = wo[pl.ds(pl.multiple_of((1 - core) * 64, 64), 64), :]
-        w = jnp.concatenate([w_own, w_other], axis=0)
-        for j in range(8):
-            a = pn[0, pl.ds(j, 128, stride=8), :].T
-            b = pn[1, pl.ds(j, 128, stride=8), :].T
-            v = jnp.concatenate([a, jnp.where(first, b[0:64], b[64:128])], axis=0)
-            v = (v * out_gain + out_shift).astype(BF)
-            u = jnp.dot(v, w, preferred_element_type=F32) * gate[t * 8 + j]
-            ostage[pl.ds(j, 192, stride=8), :] = u
-        for u in range(3):
-            out_ref[:, u, :, pl.ds(pl.multiple_of(t * 8, 8), 8), :] = (
-                ostage[u * 512 : (u + 1) * 512, :].reshape(8, 8, 8, 128).astype(BF)
-            )
-        return carry
-
-    lax.fori_loop(0, 3, finish, 0)
+        pltpu.make_async_copy(peer_p.at[pl.ds(0, 64)], peer_p.at[pl.ds(0, 64)], e_recv.at[t]).wait()
+        standardize(
+            0,
+            lambda lo, size: (
+                recv_p[pl.ds(t * 64 + lo, size), :, pl.ds(own_lane, 128)], peer_p[pl.ds(t * 64 + lo, size), :, 0:128]
+            ),
+        )
+        standardize(1, read_shared(t))
+        project_out(t, 0)
+        project_out(t, 1)
+        return carry
+
+    lax.fori_loop(0, 2, finish_early, 0)
+    last = jnp.int32(2)
+    pltpu.make_async_copy(lown.at[pl.ds(0, 63)], lown.at[pl.ds(0, 63)], p_recv.at[2]).wait()
+    to_peer(last, 1).start()
+    pltpu.make_async_copy(lown.at[pl.ds(0, 64)], lown.at[pl.ds(0, 64)], e_recv.at[2]).wait()
+    standardize(1, read_shared(last))
+    project_out(last, 1)
+    pltpu.make_async_copy(lown.at[pl.ds(0, 127)], lown.at[pl.ds(0, 127)], d_recv).wait()
+    standardize(0, lambda lo, size: (recv_d[lo : lo + size], recv_d[64 + lo : 64 + lo + size]))
+    project_out(last, 0)
 
     for t in range(3):
         for u in range(2):
             peer_copy(t, u).wait_send()
-        to_peer(t, 0).wait_send()
+        if t < 2:
+            to_peer(t, 0).wait_send()
         to_peer(t, 1).wait_send()
-    pltpu.make_async_copy(xs.at[pl.ds(0, 2272)], xs.at[pl.ds(0, 2272)], l_send).wait()
-    for sem, buf in ((r_send, rsend), (p_send, recv_p)):
-        pltpu.make_async_copy(buf.at[pl.ds(0, 189)], buf.at[pl.ds(0, 189)], sem).wait()
+    for sem in (l_send, p_send):
+        pltpu.make_async_copy(xs.at[pl.ds(0, 2272)], xs.at[pl.ds(0, 2272)], sem).wait()
+    pltpu.make_async_copy(rsend.at[pl.ds(0, 189)], rsend.at[pl.ds(0, 189)], r_send).wait()
 
 
 def per_device(pair_input, in_gain, in_shift, w_proj, w_gate, out_gain, out_shift, w_out):
@@ -366,6 +416,7 @@
             pltpu.VMEM((96, 8, 768), BF),
             pltpu.VMEM((96, 8, 768), BF),
             pltpu.VMEM((192, 8, 384), BF),
+            pltpu.VMEM((128, 8, 128), BF),
             pltpu.VMEM((192, 8, 256), BF),
             pltpu.VMEM((24, 192, 128), F32),
             pltpu.VMEM((2, 1024, 128), F32),
@@ -384,6 +435,7 @@
             dma((3,)),
             dma,
             dma((3,)),
+            dma,
             dma,
             dma((3,)),
         ],

time: 55.9 us -> 53.6 us (0.959)
  Pallas kernels: 54.8 us -> 52.4 us
    pallas_call x1, Pallas kernels: 54.8 us -> 52.4 us  [per_device(): pl.pallas_call(kernel, out_shape=pltpu.VMEM((8, 3, 8, 24, 128), BF), in_s...]
where the time goes in v4:
time: 53.6 us; the launch traced here: 53.5 us
  Pallas kernels  52.4 us (98%)
  local copies, waits for them, and re-layouts  1.02 us (2%)
    pallas_call x1, Pallas kernels, per_device(): pl.pallas_call(kernel, out_shape=pltpu.VMEM((8, 3, 8, 24, 128), BF), in_s...  52.4 us

profile of v4, /device:TPU:1, one launch (start us, length us, event | category | flops | bytes accessed | tf_op | source)
XLA Modules:
  0.0 53.5 jit_solution(12509304583330564727)
XLA Ops:
  0.0 52.4 %triangle.1 = bf16[8,3,8,24,128]{4,3,2,1,0:T(8,128)(2,1)S(1)} custom-call(bf16[8,3,8,24,128]{4,3,2,1,0:T(8,128)(2,1)} %bitcast.7, f32[1,128]{1,0:T(1,128)} %bitcast.8, f32[1,128]{1,0:T(1,128)} %bitcast.9, bf16[128,512]{1,0:T(8,128)(2,1)} %wp_ref.1, bf16[128,128]{1,0:T(8,128)(2,1)} %wg_ref.1, f32[1,128]{1,0:T(1,128)} %bitcast.10, f32[1,128]{1,0:T(1,128)} %bitcast.11, ...), custom_call_target="tpu_custom_call" | custom-call | tf_op jit(solution)/shard_map/triangle/pallas_call | solution.py:402
  52.4 1.0 %copy.10 = bf16[192,24,128]{2,1,0:T(8,128)(2,1)} copy(bf16[192,24,128]{2,1,0:T(8,128)(2,1)S(1)} %bitcast.6) | data formatting | bytes 2359296

commit v5 on v4

--- a/solution.py
+++ b/solution.py
@@ -39,7 +39,7 @@
     x_ref, ig_ref, is_ref, wp_ref, wg_ref, og_ref, os_ref, wo_ref, out_ref,
     xin, xs, wall, lown, lsend, rsend, stage, recv_l, recv_r, psend, recv_p, recv_d, peer_p,
     gate, pn, ostage, wp, wg, wo, vecs,
-    w_sem, own_sem, x_send, x_recv, l_send, l_recv, r_send, r_recv, p_send, p_recv, d_recv, e_send, e_recv,
+    w_sem, own_sem, x_send, x_recv, l_send, l_recv, r_send, r_recv, p_send, p_recv, d_recv, e_send, e_recv, ready,
 ):
     row = lax.axis_index("row")
     col = lax.axis_index("col")
@@ -91,12 +91,11 @@
         copy.start()
 
     barrier = pltpu.get_barrier_semaphore()
-    each_device(lambda n, owner, device: pl.semaphore_signal(barrier, inc=1, device_id=device), FAR)
-
-    for copy in weights:
-        copy.wait()
-    for part in range(4):
-        wall[part * 128 : (part + 1) * 128, :] = wp[:, part * 128 : (part + 1) * 128].astype(F32).T.astype(BF)
+    each_chip(lambda zh2, q2, n, device: pl.semaphore_signal(barrier, inc=1, device_id=device), FAR)
+    pl.semaphore_signal(barrier, inc=1, device_id=other)
+
+    for n in (1, 2):
+        weights[n].wait()
 
     in_gain = vecs[0]
     in_shift = vecs[1]
@@ -125,12 +124,19 @@
         return div(q, 16) * 48 + rem(div(q, 8), 2) * (16 - 8 * late) + t * 8 * (1 - late) + 32 * late + rem(q, 8)
 
     norm_own(0, 0)
+    def turn(part):
+        wall[part * 128 : (part + 1) * 128, :] = wp[:, part * 128 : (part + 1) * 128].astype(F32).T.astype(BF)
+
+    weights[0].wait()
+    turn(0)
+    turn(1)
     for i in range(8):
         rows = xs[pl.ds(core * 1024 + i, 128, stride=8), :].astype(BF)
         p = dot_nt(wall[0:256, :], rows)
         pn[0, pl.ds(i, 128, stride=8), :] = jax.nn.sigmoid(p[0:128]) * p[128:256]
     lown[...] = pn[0].reshape(128, 8, 128).astype(BF)
-    pl.semaphore_wait(barrier, 127)
+    pl.semaphore_wait(barrier, 64)
+    pl.semaphore_signal(ready, inc=1, device_id=other)
 
     def peer_copy(t, u):
         here = pl.ds(core * 16, 16) if u == 0 else pl.ds(32 + core * 8, 8)
@@ -160,7 +166,9 @@
             device_id=device,
         ).start()
 
-    each_device(send_own, ORDER)
+    each_chip(lambda zh2, q2, n, device: send_own(n, core, device))
+    pl.semaphore_wait(ready, 1)
+    each_device(lambda n, owner, device: send_own(n, owner, device) if owner is not core else None, ORDER)
     recv_l[group, :, own_tile] = lown[core * 64 + me]
 
     def widen_peer(t):
@@ -215,6 +223,11 @@
         return carry
 
     lax.fori_loop(1, 3, left_all, 0)
+
+    turn(2)
+    turn(3)
+    for n in (3, 4, 5, 6):
+        weights[n].wait()
 
     def right(t, carry):
         project(t, 2, rsend, (0, 1, 2))
@@ -438,6 +451,7 @@
             dma,
             dma,
             dma((3,)),
+            pltpu.SemaphoreType.REGULAR,
         ],
         compiler_params=pltpu.CompilerParams(
             collective_id=0, has_side_effects=True, vmem_limit_bytes=int(54 * 2**20)

time: 53.6 us -> 53.3 us (level)
  no operation moved by 1% of the time
where the time goes in v5:
time: 53.3 us; the launch traced here: 53.2 us
  Pallas kernels  52.2 us (98%)
  local copies, waits for them, and re-layouts  1.02 us (2%)
    pallas_call x1, Pallas kernels, per_device(): pl.pallas_call(kernel, out_shape=pltpu.VMEM((8, 3, 8, 24, 128), BF), in_s...  52.2 us

profile of v5, /device:TPU:1, one launch (start us, length us, event | category | flops | bytes accessed | tf_op | source)
XLA Modules:
  0.0 53.2 jit_solution(11019728548706701726)
XLA Ops:
  0.0 52.2 %triangle.1 = bf16[8,3,8,24,128]{4,3,2,1,0:T(8,128)(2,1)S(1)} custom-call(bf16[8,3,8,24,128]{4,3,2,1,0:T(8,128)(2,1)} %bitcast.7, f32[1,128]{1,0:T(1,128)} %bitcast.8, f32[1,128]{1,0:T(1,128)} %bitcast.9, bf16[128,512]{1,0:T(8,128)(2,1)} %wp_ref.1, bf16[128,128]{1,0:T(8,128)(2,1)} %wg_ref.1, f32[1,128]{1,0:T(1,128)} %bitcast.10, f32[1,128]{1,0:T(1,128)} %bitcast.11, ...), custom_call_target="tpu_custom_call" | custom-call | tf_op jit(solution)/shard_map/triangle/pallas_call | solution.py:415
  52.2 1.0 %copy.10 = bf16[192,24,128]{2,1,0:T(8,128)(2,1)} copy(bf16[192,24,128]{2,1,0:T(8,128)(2,1)S(1)} %bitcast.6) | data formatting | bytes 2359296
